TPU v7x, 32 devices: a whole 2x2x4 slice. The times are simulated.
32 devices in a mesh: gx: 2 (over x), gy: 4 (over z), gz: 4 (over y, core).
Axes of the slice: x: 2, y: 2, z: 4, core: 2. Of those that a mesh axis runs over, the one named last changes fastest.
Arguments:
- calcium: float32 [8, 64, 128, 512], P(None, 'gx', 'gz', 'gy'), may hold values from 0.1 to 3
- activation: float32 [8, 64, 128, 512], P(None, 'gx', 'gz', 'gy'), may hold values from 0 to 1
- element_first: int32 [64], replicated, may hold values from 0 to 15, as said below
- offset_first: float32 [64], replicated, may hold values from 0.1 to 0.9
- element_second: int32 [512], replicated, may hold values from 0 to 127, as said below
- offset_second: float32 [512], replicated, may hold values from 0.1 to 0.9
- element_third: int32 [128], replicated, may hold values from 0 to 31, as said below
- offset_third: float32 [128], replicated, may hold values from 0.1 to 0.9
- troponin: float32 [16, 32, 128], P('gx', ('gy', 'gz')), may hold values from 0 to 1
- tension: float32 [16, 32, 128], P('gx', ('gy', 'gz')), may hold values from 0 to 2
- unbind_rate: float32 [16, 32, 128], P('gx', ('gy', 'gz')), may hold values from 0.2 to 2
- relax_rate: float32 [16, 32, 128], P('gx', ('gy', 'gz')), may hold values from 0.5 to 4
Outputs:
- bound_fraction: float32 [16, 32, 128], P('gx', ('gy', 'gz'))
- active_tension: float32 [16, 32, 128], P('gx', ('gy', 'gz'))
Inputs may be any that keep to these rules, and one draw needn't show every extreme that they name: `element_first`: never falling; the cells of each aligned block of 32 cells belong to that block's own 8 elements, each element holding at least one cell. `element_second`: never falling; the cells of each aligned block of 128 cells belong to that block's own 32 elements, each element holding at least one cell. `element_third`: never falling; the cells of each aligned block of 8 cells belong to that block's own 2 elements, each element holding at least one cell.
All inputs are finite; a program needn't handle non-finite values.
Results may differ from a plain program's by a relative error of at most 0.00005.
Values sent between devices are 32-bit elements.
A program may use at most 64 MiB of HBM per device.

v0:
```python
import jax
import jax.numpy as jnp
from jax import lax
from jax.sharding import PartitionSpec as P

highest = lax.Precision.HIGHEST
step_size = 0.2
bind_rate = 2.0
peak_tension = 2.0
half_square = 0.25


def shifted(x, axis, by):
    length = lax.axis_size(axis)
    pairs = [(i, i + by) for i in range(length) if 0 <= i + by < length]
    return lax.ppermute(x, axis, pairs)


def axis_weights(element, offset, first_node, count, first_cell, cells):
    node_ids = first_node + jnp.arange(count, dtype=jnp.int32)
    inside = element[None, :] == node_ids[:, None]
    following = element[None, :] + 1 == node_ids[:, None]
    raw_weights = jnp.where(inside, 1.0 - offset[None, :], 0.0) + jnp.where(
        following, offset[None, :], 0.0
    )
    scaled = raw_weights / jnp.sum(raw_weights, axis=1, keepdims=True)
    return lax.dynamic_slice_in_dim(scaled, first_cell, cells, 1)


def restrict_block(field, weight_row, weight_depth, weight_col):
    section = jnp.einsum("ai,sizy->sazy", weight_row, field, precision=highest)
    section = jnp.einsum("bz,sazy->saby", weight_depth, section, precision=highest)
    return jnp.einsum("cy,saby->sabc", weight_col, section, precision=highest)


def last_layer(partial_value, dim):
    extent = partial_value.shape[dim]
    return lax.slice_in_dim(partial_value, extent - 1, extent, axis=dim)


def merge_edge(partial_value, incoming, dim):
    extent = partial_value.shape[dim]
    leading = lax.slice_in_dim(partial_value, 0, 1, axis=dim) + incoming
    middle = lax.slice_in_dim(partial_value, 1, extent - 1, axis=dim)
    return lax.concatenate([leading, middle], dim)


def fold_rows(partial_value):
    incoming = shifted(last_layer(partial_value, 2), "gx", 1)
    return merge_edge(partial_value, incoming, 2)


def tension_steps(drivers, troponin, tension, unbind_rate, relax_rate):
    bound = troponin
    active = tension
    for substep in range(drivers.shape[1]):
        calcium_now = drivers[0, substep]
        squared = calcium_now * calcium_now
        binding = squared / (squared + half_square)
        bound = bound + step_size * (bind_rate * binding * (1.0 - bound) - unbind_rate * bound)
        active = active + step_size * relax_rate * (
            peak_tension * drivers[1, substep] * bound - active
        )
    return (bound, active)


def per_device(
    calcium,
    activation,
    element_first,
    offset_first,
    element_second,
    offset_second,
    element_third,
    offset_third,
    troponin,
    tension,
    unbind_rate,
    relax_rate,
):
    sub_count, fine_rows, fine_depth, fine_cols = calcium.shape
    nodes_x, nodes_block, nodes_all_y = troponin.shape
    groups = lax.axis_size("gz")
    row_index = lax.axis_index("gx")
    weight_row = axis_weights(
        element_first,
        offset_first,
        row_index * nodes_x,
        nodes_x + 1,
        row_index * fine_rows,
        fine_rows,
    )
    slab_index = lax.axis_index("gz")
    col_index = lax.axis_index("gy")
    slab_nodes = nodes_block * groups
    nodes_y = nodes_all_y // lax.axis_size("gy")
    weight_depth = axis_weights(
        element_third,
        offset_third,
        slab_index * slab_nodes,
        slab_nodes + 1,
        slab_index * fine_depth,
        fine_depth,
    )
    weight_col = axis_weights(
        element_second,
        offset_second,
        col_index * nodes_y,
        nodes_y + 1,
        col_index * fine_cols,
        fine_cols,
    )
    partial_value = jnp.stack(
        [
            restrict_block(field, weight_row, weight_depth, weight_col)
            for field in (calcium, activation)
        ]
    )
    partial_value = fold_rows(partial_value)
    incoming = shifted(last_layer(partial_value, 3), "gz", 1)
    partial_value = merge_edge(partial_value, incoming, 3)
    incoming = shifted(last_layer(partial_value, 4), "gy", 1)
    partial_value = merge_edge(partial_value, incoming, 4)
    shaped = partial_value.reshape(2, 1, sub_count, nodes_x, groups, nodes_block, nodes_y)
    regrouped = lax.all_to_all(
        lax.all_to_all(shaped, "gz", split_axis=4, concat_axis=1, tiled=True),
        "gy",
        split_axis=1,
        concat_axis=6,
        tiled=True,
    )
    drivers = regrouped.reshape(2, sub_count, nodes_x, nodes_block, nodes_all_y)
    return tension_steps(drivers, troponin, tension, unbind_rate, relax_rate)


def solution(mesh):
    return jax.shard_map(
        per_device,
        mesh=mesh,
        in_specs=(
            P(None, "gx", "gz", "gy"),
            P(None, "gx", "gz", "gy"),
            P(),
            P(),
            P(),
            P(),
            P(),
            P(),
            P("gx", ("gy", "gz"), None),
            P("gx", ("gy", "gz"), None),
            P("gx", ("gy", "gz"), None),
            P("gx", ("gy", "gz"), None),
        ),
        out_specs=(P("gx", ("gy", "gz"), None), P("gx", ("gy", "gz"), None)),
        check_vma=False,
    )
```

profile of v0, /device:TPU:0, one launch (start us, length us, event | category | flops | bytes accessed | tf_op | source)
XLA Modules:
  0.0 75.7 jit_solution(12411351892337672880)
XLA Ops:
  0.6 0.7 broadcast_add_fusion.2
  1.3 0.7 broadcast_subtract_fusion.2
  2.0 0.7 broadcast_add_fusion.1
  2.6 0.7 broadcast_subtract_fusion.1
  3.3 0.7 broadcast_add_fusion
  4.0 0.7 broadcast_subtract_fusion
  4.7 0.9 %fusion.127 = (f32[9]{0:T(128)S(1)}, f32[9,64]{1,0:T(8,128)S(1)}) fusion(f32[64]{0:T(128)} %param.15, s32[64]{0:T(128)S(1)} %broadcast_add_fusion.2, f32[64]{0:T(128)S(1)} %broadcast_subtract_fusion.2, s32[9]{0:T(128)S(1)} %iota_add_fusion.2, s32[64]{0:T(128)} %param.14), kind=kLoop, calls=%fused_computation.170 | loop fusion | flops 3447 | bytes 3400 | tf_op jit(solution)/shard_map/reduce_sum | solution.py:26
  5.5 0.0 copy-start
  5.5 7.9 %fusion.4 = f32[8,9,32,128]{3,1,2,0:T(8,128)} fusion(f32[8,32,32,128]{3,2,1,0:T(8,128)} %param.12, f32[9,64]{1,0:T(8,128)S(1)} %get-tuple-element.11, s32[]{:T(128)S(6)} %select_n.32, f32[9]{0:T(128)S(1)} %get-tuple-element.10), kind=kOutput, calls=%fused_computation.4 | convolution fusion | flops 113246496 | bytes 5376296 | tf_op jit(solution)/shard_map/ai,sizy->sazy/dot_general | solution.py:31
  13.5 0.0 copy-done
  13.5 0.0 copy-start.7
  13.5 0.0 copy-start.8
  13.5 4.4 %fusion.7 = f32[8,9,32,128]{3,1,2,0:T(8,128)S(1)} fusion(f32[8,32,32,128]{3,2,1,0:T(8,128)S(1)} %copy-done, f32[9,64]{1,0:T(8,128)S(1)} %get-tuple-element.11, s32[]{:T(128)S(6)} %select_n.32, f32[9]{0:T(128)S(1)} %get-tuple-element.10), kind=kOutput, calls=%fused_computation.5 | convolution fusion | flops 113246496 | bytes 5376296 | tf_op jit(solution)/shard_map/ai,sizy->sazy/dot_general | solution.py:31
  17.8 0.0 copy-start.5
  17.9 0.0 copy-start.6
  17.9 0.0 copy-done.7
  17.9 0.0 copy-done.8
  17.9 0.2 fusion.128
  18.1 2.6 %convolution_bitcast_fusion.3 = f32[8,9,9,128]{3,2,1,0:T(8,128)S(1)} fusion(f32[8,9,32,128]{3,1,2,0:T(8,128)} %fusion.4, f32[9,128]{1,0:T(8,128)S(1)} %get-tuple-element.9, s32[]{:T(128)S(6)} %select_n.35, f32[9]{0:T(128)S(1)} %get-tuple-element.8), kind=kOutput, calls=%fused_computation.9 | convolution fusion | flops 31850784 | bytes 1516072 | tf_op jit(solution)/shard_map/bz,sazy->saby/dot_general | solution.py:32
  20.7 1.1 %convolution_bitcast_fusion.1 = f32[8,9,9,128]{3,2,1,0:T(8,128)S(1)} fusion(f32[8,9,32,128]{3,1,2,0:T(8,128)S(1)} %fusion.7, f32[9,128]{1,0:T(8,128)S(1)} %get-tuple-element.9, s32[]{:T(128)S(6)} %select_n.35, f32[9]{0:T(128)S(1)} %get-tuple-element.8), kind=kOutput, calls=%fused_computation.7 | convolution fusion | flops 31850784 | bytes 1516072 | tf_op jit(solution)/shard_map/bz,sazy->saby/dot_general | solution.py:32
  21.8 0.0 copy-done.5
  21.8 0.0 copy-done.6
  21.8 0.2 fusion.112
  22.0 0.9 %convolution_bitcast_fusion.2 = f32[1,8,9,9,33]{4,3,2,1,0:T(8,128)S(1)} fusion(f32[8,9,9,128]{3,2,1,0:T(8,128)S(1)} %convolution_bitcast_fusion.3, f32[33,512]{1,0:T(8,128)S(1)} %get-tuple-element.7, s32[]{:T(128)S(6)} %select_n.38, f32[33]{0:T(128)S(1)} %get-tuple-element.6), kind=kOutput, calls=%fused_computation.8 | convolution fusion | flops 32850048 | bytes 696356 | tf_op jit(solution)/shard_map/cy,saby->sabc/dot_general | solution.py:33
  22.9 0.7 convolution_bitcast_fusion
  23.6 4.9 %collective-permute-start = (f32[2,8,1,9,33]{4,3,2,1,0:T(8,128)S(1)}, f32[2,8,1,9,33]{4,3,2,1,0:T(8,128)S(1)}, u32[]{:S(2)}, u32[]{:S(2)}) collective-permute-start(f32[2,8,1,9,33]{4,3,2,1,0:T(8,128)S(1)} %pad_maximum_fusion), channel_id=1, source_target_pairs={{0,16},{1,17},{2,18},{3,19},{4,20},{5,21},{6,22},{7,23},{8,24},{9,... | collective-permute-start | bytes 57032 | tf_op jit(solution)/shard_map/ppermute | solution.py:16
  28.5 2.7 %collective-permute-done = f32[2,8,1,9,33]{4,3,2,1,0:T(8,128)S(1)} collective-permute-done((f32[2,8,1,9,33]{4,3,2,1,0:T(8,128)S(1)}, f32[2,8,1,9,33]{4,3,2,1,0:T(8,128)S(1)}, u32[]{:S(2)}, u32[]{:S(2)}) %collective-permute-start) | collective-permute-done | bytes 19040 | tf_op jit(solution)/shard_map/ppermute | solution.py:16
  31.2 0.1 fusion.12
  31.4 1.3 %collective-permute-start.1 = (f32[2,8,8,1,33]{4,3,2,1,0:T(1,128)S(1)}, f32[2,8,8,1,33]{4,3,2,1,0:T(1,128)S(1)}, u32[]{:S(2)}, u32[]{:S(2)}) collective-permute-start(f32[2,8,8,1,33]{4,3,2,1,0:T(1,128)S(1)} %slice.101), channel_id=1, source_target_pairs={{0,1},{1,2},{2,3},{4,5},{5,6},{6,7},{8,9},{9,10},{10,11},{12,13},{... | collective-permute-start | bytes 50696 | tf_op jit(solution)/shard_map/ppermute | solution.py:16
  32.7 0.1 slice.102
  32.7 0.8 %collective-permute-done.1 = f32[2,8,8,1,33]{4,3,2,1,0:T(1,128)S(1)} collective-permute-done((f32[2,8,8,1,33]{4,3,2,1,0:T(1,128)S(1)}, f32[2,8,8,1,33]{4,3,2,1,0:T(1,128)S(1)}, u32[]{:S(2)}, u32[]{:S(2)}) %collective-permute-start.1) | collective-permute-done | bytes 16928 | tf_op jit(solution)/shard_map/ppermute | solution.py:16
  33.6 0.1 slice_add_fusion
  33.6 0.3 fusion.13
  34.0 3.5 %collective-permute-start.2 = (f32[2,8,8,8,1]{4,3,2,1,0:T(8,128)S(1)}, f32[2,8,8,8,1]{4,3,2,1,0:T(8,128)S(1)}, u32[]{:S(2)}, u32[]{:S(2)}) collective-permute-start(f32[2,8,8,8,1]{4,3,2,1,0:T(8,128)S(1)} %fusion.13), channel_id=1, source_target_pairs={{0,4},{4,8},{8,12},{1,5},{5,9},{9,13},{2,6},{6,10},{10,14},{3,7},{... | collective-permute-start | bytes 12296 | tf_op jit(solution)/shard_map/ppermute | solution.py:16
  37.5 10.6 %collective-permute-done.2 = f32[2,8,8,8,1]{4,3,2,1,0:T(8,128)S(1)} collective-permute-done((f32[2,8,8,8,1]{4,3,2,1,0:T(8,128)S(1)}, f32[2,8,8,8,1]{4,3,2,1,0:T(8,128)S(1)}, u32[]{:S(2)}, u32[]{:S(2)}) %collective-permute-start.2) | collective-permute-done | bytes 4128 | tf_op jit(solution)/shard_map/ppermute | solution.py:16
  48.1 0.1 fusion.15
  48.2 0.2 fusion.16
  48.4 0.2 copy.103
  48.6 0.5 reshape.73
  49.2 8.9 %all_to_all.33 = f32[4,1,8192]{2,1,0:T(1,128)S(1)} all-to-all(f32[4,1,8192]{2,1,0:T(1,128)S(1)} %reshape.73), channel_id=1, replica_groups=mesh['gx'=2,'gy'=4,'gz'=4] {'gz'}, dimensions={0} | all-to-all | bytes 262144 | tf_op jit(solution)/shard_map/all_to_all | solution.py:126
  58.1 0.5 broadcast.223
  58.6 1.0 %reduce = f32[4,8192]{1,0:T(4,128)S(1)} reduce(f32[4,1,8192]{2,1,0:T(1,128)S(1)} %all_to_all.33, f32[]{:T(128)} %broadcast.223), dimensions={1}, to_apply=%all_to_all.24.reduce_sub_computation | reduce | bytes 262148 | tf_op jit(solution)/shard_map/all_to_all | solution.py:126
  59.6 0.5 reshape.74
  60.1 0.5 reshape.75
  60.6 0.0 copy-start.1
  60.6 0.0 copy-start.2
  60.6 0.0 copy-start.3
  60.7 0.0 copy-start.4
  60.7 11.6 %all_to_all.34 = f32[4,1,8192]{2,1,0:T(1,128)S(1)} all-to-all(f32[4,1,8192]{2,1,0:T(1,128)S(1)} %reshape.75), channel_id=1, replica_groups=mesh['gx'=2,'gy'=4,'gz'=4] {'gy'}, dimensions={0} | all-to-all | bytes 262144 | tf_op jit(solution)/shard_map/all_to_all | solution.py:125
  72.3 1.0 %reduce.1 = f32[4,8192]{1,0:T(4,128)S(1)} reduce(f32[4,1,8192]{2,1,0:T(1,128)S(1)} %all_to_all.34, f32[]{:T(128)} %broadcast.223), dimensions={1}, to_apply=%all_to_all.28.reduce_sub_computation | reduce | bytes 262148 | tf_op jit(solution)/shard_map/all_to_all | solution.py:125
  73.3 0.5 reshape.76
  73.8 0.3 copy.23
  74.1 0.3 reshape.69
  74.4 0.0 copy-done.1
  74.4 0.0 copy-done.2
  74.4 0.0 copy-done.3
  74.4 0.0 copy-done.4
  74.4 0.1 fusion.66
  74.5 0.6 copy.38
  75.1 0.6 copy.39
  (8 shorter events, 0.2 us)
Async XLA Ops:
  5.5 7.9 %copy-start = (f32[8,32,32,128]{3,2,1,0:T(8,128)S(1)}, f32[8,32,32,128]{3,2,1,0:T(8,128)}, u32[]{:S(2)}) copy-start(f32[8,32,32,128]{3,2,1,0:T(8,128)} %param.13) | copy-start | bytes 12582916
  13.5 4.4 %copy-start.7 = (f32[128]{0:T(128)S(1)}, f32[128]{0:T(128)}, u32[]{:S(2)}) copy-start(f32[128]{0:T(128)} %param.19) | copy-start | bytes 1540
  13.5 4.4 %copy-start.8 = (s32[128]{0:T(128)S(1)}, s32[128]{0:T(128)}, u32[]{:S(2)}) copy-start(s32[128]{0:T(128)} %param.18) | copy-start | bytes 1540
  17.8 3.9 %copy-start.5 = (f32[512]{0:T(512)S(1)}, f32[512]{0:T(512)}, u32[]{:S(2)}) copy-start(f32[512]{0:T(512)} %param.17) | copy-start | bytes 6148
  17.9 3.9 %copy-start.6 = (s32[512]{0:T(512)S(1)}, s32[512]{0:T(512)}, u32[]{:S(2)}) copy-start(s32[512]{0:T(512)} %param.16) | copy-start | bytes 6148
  23.6 7.6 %collective-permute-start = (f32[2,8,1,9,33]{4,3,2,1,0:T(8,128)S(1)}, f32[2,8,1,9,33]{4,3,2,1,0:T(8,128)S(1)}, u32[]{:S(2)}, u32[]{:S(2)}) collective-permute-start(f32[2,8,1,9,33]{4,3,2,1,0:T(8,128)S(1)} %pad_maximum_fusion), channel_id=1, source_target_pairs={{0,16},{1,17},{2,18},{3,19},{4,20},{5,21},{6,22},{7,23},{8,24},{9,... | collective-permute-start | bytes 57032 | tf_op jit(solution)/shard_map/ppermute | solution.py:16
  31.4 2.2 %collective-permute-start.1 = (f32[2,8,8,1,33]{4,3,2,1,0:T(1,128)S(1)}, f32[2,8,8,1,33]{4,3,2,1,0:T(1,128)S(1)}, u32[]{:S(2)}, u32[]{:S(2)}) collective-permute-start(f32[2,8,8,1,33]{4,3,2,1,0:T(1,128)S(1)} %slice.101), channel_id=1, source_target_pairs={{0,1},{1,2},{2,3},{4,5},{5,6},{6,7},{8,9},{9,10},{10,11},{12,13},{... | collective-permute-start | bytes 50696 | tf_op jit(solution)/shard_map/ppermute | solution.py:16
  34.0 14.1 %collective-permute-start.2 = (f32[2,8,8,8,1]{4,3,2,1,0:T(8,128)S(1)}, f32[2,8,8,8,1]{4,3,2,1,0:T(8,128)S(1)}, u32[]{:S(2)}, u32[]{:S(2)}) collective-permute-start(f32[2,8,8,8,1]{4,3,2,1,0:T(8,128)S(1)} %fusion.13), channel_id=1, source_target_pairs={{0,4},{4,8},{8,12},{1,5},{5,9},{9,13},{2,6},{6,10},{10,14},{3,7},{... | collective-permute-start | bytes 12296 | tf_op jit(solution)/shard_map/ppermute | solution.py:16
  60.6 13.8 %copy-start.1 = (f32[8,2,128]{2,1,0:T(2,128)S(1)}, f32[8,2,128]{2,1,0:T(2,128)}, u32[]{:S(2)}) copy-start(f32[8,2,128]{2,1,0:T(2,128)} %param.21) | copy-start | bytes 24580
  60.6 13.8 %copy-start.2 = (f32[8,2,128]{2,1,0:T(2,128)S(1)}, f32[8,2,128]{2,1,0:T(2,128)}, u32[]{:S(2)}) copy-start(f32[8,2,128]{2,1,0:T(2,128)} %param.23) | copy-start | bytes 24580
  60.6 13.8 %copy-start.3 = (f32[8,2,128]{2,1,0:T(2,128)S(1)}, f32[8,2,128]{2,1,0:T(2,128)}, u32[]{:S(2)}) copy-start(f32[8,2,128]{2,1,0:T(2,128)} %param.22) | copy-start | bytes 24580
  60.7 13.8 %copy-start.4 = (f32[8,2,128]{2,1,0:T(2,128)S(1)}, f32[8,2,128]{2,1,0:T(2,128)}, u32[]{:S(2)}) copy-start(f32[8,2,128]{2,1,0:T(2,128)} %param.20) | copy-start | bytes 24580
where the time goes:
time: 76.1 us; the launch traced here: 75.7 us
  blocking collectives  20.5 us (27%)
  matrix products  17.6 us (23%)
  waiting for transfers between devices  14.1 us (19%)
  starting transfers between devices  9.68 us (13%)
  other arithmetic  8.15 us (11%)
  local copies, waits for them, and re-layouts  4.72 us (6%)
  between operations  0.96 us (1%)
    ppermute x3, waiting for transfers between devices, shifted(): return lax.ppermute(x, axis, pairs)  14.1 us
    dot_general x2, matrix products, restrict_block(): section = jnp.einsum('ai,sizy->sazy', weight_row, field, precision=highest)  12.3 us
    all_to_all x1, blocking collectives, per_device(): lax.all_to_all(lax.all_to_all(shaped, 'gz', split_axis=4, concat_axis=1,...  11.6 us
    ppermute x3, starting transfers between devices, shifted(): return lax.ppermute(x, axis, pairs)  9.68 us
    all_to_all x1, blocking collectives, per_device(): lax.all_to_all(shaped, 'gz', split_axis=4, concat_axis=1, tiled=True)  8.91 us
    dot_general x2, matrix products, restrict_block(): jnp.einsum('bz,sazy->saby', weight_depth, section, precision=highest)  3.68 us
    unnamed x25, local copies, waits for them, and re-layouts  3.29 us
    add x3, other arithmetic, axis_weights(): following = element[None, :] + 1 == node_ids[:, None]  2 us
  transfers between devices with their start and end apart: 3, of which 3 were waited for; matrix products, arithmetic and copies ran while one was open for 0% of the time, Pallas kernels for 0%

commit v1 on v0

v1 whole, which is shorter than its diff:
```python
import functools

import jax
import jax.numpy as jnp
from jax import lax
from jax.experimental import pallas as pl
from jax.experimental.pallas import tpu as pltpu
from jax.sharding import PartitionSpec as P

step_size = 0.2
bind_rate = 2.0
peak_tension = 2.0
half_square = 0.25
f32 = jnp.float32
bf16 = jnp.bfloat16
MESH = pl.DeviceIdType.MESH
CHUNKS = 2


def split(x):
    high = x.astype(bf16)
    return high, (x - high.astype(f32)).astype(bf16)


def node_weights(element, offset, node):
    raw = jnp.where(element == node, 1.0 - offset, 0.0) + jnp.where(
        element + 1 == node, offset, 0.0
    )
    total = jnp.sum(raw, axis=1, keepdims=True)
    return raw, jnp.where(total > 0.0, total, 1.0)


def iota(shape, dim):
    return lax.broadcasted_iota(jnp.int32, shape, dim)


def kernel(
    calcium,
    activation,
    e1,
    o1,
    e2,
    o2,
    e3,
    o3,
    troponin,
    tension,
    unbind,
    relax,
    out_bound,
    out_active,
    xc,
    xa,
    main,
    edge,
    got_main,
    got_third,
    got_first,
    got_corner,
    load_sem,
    send_main,
    send_edge,
    recv_main,
    recv_third,
    recv_first,
    recv_corner,
    *,
    sizes,
):
    nx, ny, nz = sizes
    subs, rows, depth, cols = xc.shape
    nodes_x, per_block, all_y = troponin.shape
    nodes_y = all_y // ny
    blocks = nz
    slab = per_block * blocks
    gx, gy, gz = lax.axis_index("gx"), lax.axis_index("gy"), lax.axis_index("gz")
    chunk = subs // CHUNKS

    def load(t):
        return (
            pltpu.make_async_copy(calcium.at[t], xc.at[t], load_sem.at[0, t]),
            pltpu.make_async_copy(activation.at[t], xa.at[t], load_sem.at[1, t]),
        )

    for t in range(subs):
        for copy in load(t):
            copy.start()

    barrier = pltpu.get_barrier_semaphore()
    has_next_x = gx + 1 < nx
    has_next_z = gz + 1 < nz
    own = gy == gz
    from_third = jnp.logical_and(gz == 0, gy > 0)
    from_first = gx > 0
    from_corner = jnp.logical_and(from_third, from_first)
    for s in range(ny):

        def greet(dx, dz, s=s):
            pl.semaphore_signal(
                barrier, inc=1, device_id=(gx - dx, s, gy - dz), device_id_type=MESH
            )

        @pl.when(jnp.logical_not(jnp.logical_and(s == gy, own)))
        def _():
            greet(0, 0)

        @pl.when(jnp.logical_and(from_third, jnp.logical_not(jnp.logical_and(s == gy, gy - 1 == gz))))
        def _():
            greet(0, 1)

        @pl.when(from_first)
        def _():
            greet(1, 0)

        @pl.when(from_corner)
        def _():
            greet(1, 1)

    row_count = (slab + 1) * nodes_x + 16
    r = iota((row_count, 1), 0)
    inner = r < (slab + 1) * nodes_x
    tail = r - (slab + 1) * nodes_x
    node_a = jnp.where(inner, r % nodes_x, nodes_x)
    node_b = jnp.where(inner, r // nodes_x, per_block * (tail % 8) + tail // 8)
    raw, total = node_weights(e1[...], o1[...], node_a + gx * nodes_x)
    wide = rows * depth
    pick = (
        iota((raw.shape[1], wide), 0) == gx * rows + iota((raw.shape[1], wide), 1) // depth
    ).astype(f32)
    weight_x = jnp.dot(
        raw / total, pick, precision=lax.Precision.HIGHEST, preferred_element_type=f32
    )
    raw, total = node_weights(e3[...], o3[...], node_b + gz * slab)
    pick = (
        iota((raw.shape[1], wide), 0) == gz * depth + iota((raw.shape[1], wide), 1) % depth
    ).astype(f32)
    weight_z = jnp.dot(
        raw / total, pick, precision=lax.Precision.HIGHEST, preferred_element_type=f32
    )
    k_high, k_low = split(weight_x * weight_z)
    k_both = jnp.concatenate([k_high, k_low], axis=0)

    lanes = 2 * per_block * nodes_y
    n = iota((lanes, 1), 0)
    mine = pl.ds(pl.multiple_of(gy * cols, cols), cols)
    spread = []
    for ghost in range(2):
        node = gy * nodes_y + (nodes_y if ghost else n % nodes_y)
        node = node + jnp.zeros_like(n)
        total = node_weights(e2[...], o2[...], node)[1]
        weight = node_weights(e2[:, mine], o2[:, mine], node)[0] / total
        if ghost:
            weight = jnp.where(n % nodes_y == 0, weight, 0.0)
        spread.append(
            jnp.concatenate(
                [
                    jnp.where(n // nodes_y == f * per_block + b, weight, 0.0)
                    for b in range(per_block)
                    for f in range(2)
                ],
                axis=1,
            )
        )
    y_high, y_low = split(jnp.concatenate(spread, axis=0))

    def to_message(values):
        high, low = split(values)
        dims = (((1,), (1,)), ((), ()))
        dot = functools.partial(
            lax.dot_general, dimension_numbers=dims, preferred_element_type=f32
        )
        return dot(high, y_high) + dot(low, y_high) + dot(high, y_low)

    def part(c):
        first = c * chunk * nodes_x
        last = (c + 1) * chunk * nodes_x + (nodes_x if c == CHUNKS - 1 else 0)
        return pl.ds(first, last - first)

    def main_copy(q, c):
        return pltpu.make_async_remote_copy(
            src_ref=main.at[q, part(c)],
            dst_ref=got_main.at[gy, part(c)],
            send_sem=send_main.at[q, c],
            recv_sem=recv_main.at[gy, c],
            device_id=(gx, gz, q),
            device_id_type=MESH,
        )

    def third_copy(c):
        return pltpu.make_async_remote_copy(
            src_ref=main.at[blocks, part(c)],
            dst_ref=got_third.at[gy, part(c)],
            send_sem=send_main.at[blocks, c],
            recv_sem=recv_third.at[gy, c],
            device_id=(gx, gz + 1, 0),
            device_id_type=MESH,
        )

    def first_copy(q):
        return pltpu.make_async_remote_copy(
            src_ref=edge.at[q],
            dst_ref=got_first.at[gy],
            send_sem=send_edge.at[q],
            recv_sem=recv_first.at[gy],
            device_id=(gx + 1, gz, q),
            device_id_type=MESH,
        )

    def corner_copy():
        return pltpu.make_async_remote_copy(
            src_ref=edge.at[blocks],
            dst_ref=got_corner.at[gy],
            send_sem=send_edge.at[blocks],
            recv_sem=recv_corner.at[gy],
            device_id=(gx + 1, gz + 1, 0),
            device_id_type=MESH,
        )

    third_here = jnp.logical_and(gz == 0, gy == 1)
    third_away = jnp.logical_and(has_next_z, jnp.logical_not(third_here))

    def each_main(c, do):
        for q in range(blocks):

            @pl.when(jnp.logical_not(jnp.logical_and(own, gz == q)))
            def _(q=q):
                do(main_copy(q, c))

        @pl.when(third_away)
        def _():
            do(third_copy(c))

    def each_edge(do):
        @pl.when(has_next_x)
        def _():
            for q in range(blocks):
                do(first_copy(q))

        @pl.when(jnp.logical_and(has_next_x, has_next_z))
        def _():
            do(corner_copy())

    packed = None
    tile = nodes_x
    for c in range(CHUNKS):
        gathered = []
        for t in range(c * chunk, (c + 1) * chunk):
            for copy in load(t):
                copy.wait()
            field = jnp.concatenate(
                [xc[t].reshape(wide, cols), xa[t].reshape(wide, cols)], axis=1
            )
            high, low = split(field)
            both = jnp.dot(k_both, high, preferred_element_type=f32)
            node = (
                both[:row_count]
                + both[row_count:]
                + jnp.dot(k_high, low, preferred_element_type=f32)
            )
            sides = []
            for k in range(per_block):
                pieces = []
                for q in range(blocks + 1):
                    b = q * per_block + k
                    if b <= slab:
                        pieces.append(node[b * tile : (b + 1) * tile])
                    else:
                        pieces.append(jnp.zeros((tile, 2 * cols), f32))
                base = (slab + 1) * tile + 8 * k
                pieces.append(node[base : base + 8])
                sides.append(jnp.concatenate(pieces, axis=0))
            gathered.append(jnp.concatenate(sides, axis=1))
        result = to_message(jnp.concatenate(gathered, axis=0))
        per = (blocks + 1) * tile + 8
        for k, t in enumerate(range(c * chunk, (c + 1) * chunk)):
            values = result[k * per : (k + 1) * per]
            for q in range(blocks + 1):
                main[q, t * tile : (t + 1) * tile] = values[q * tile : (q + 1) * tile, :lanes]
                row = (blocks + 1) * tile + q
                edge[q, t : t + 1] = values[row : row + 1, :lanes]
                edge[q, subs + t : subs + t + 1] = values[row : row + 1, lanes:]
            ghost = values[: (blocks + 1) * tile, lanes:]
            if t:
                ghost = pltpu.roll(ghost, t, 1)
            packed = ghost if packed is None else packed + ghost
        if c == CHUNKS - 1:
            for q in range(blocks + 1):
                main[q, subs * tile : (subs + 1) * tile] = packed[q * tile : (q + 1) * tile]
        if c == 0:
            count = blocks + has_next_z.astype(jnp.int32)
            count = count * jnp.where(has_next_x, 2, 1)
            count = count - jnp.logical_or(own, third_here).astype(jnp.int32)
            pl.semaphore_wait(barrier, count)
        each_main(c, lambda copy: copy.start())
    each_edge(lambda copy: copy.start())

    @pl.when(own)
    def _():
        got_main[gy] = main[gz]

    @pl.when(third_here)
    def _():
        got_third[gy] = main[blocks]

    first_rows = [pl.ds(t * tile, 1) for t in range(subs)]
    for s in range(ny):

        @pl.when(jnp.logical_not(jnp.logical_and(own, gy == s)))
        def _(s=s):
            for c in range(CHUNKS):
                pltpu.make_async_remote_copy(
                    src_ref=main.at[0, part(c)],
                    dst_ref=got_main.at[s, part(c)],
                    send_sem=send_main.at[0, c],
                    recv_sem=recv_main.at[s, c],
                    device_id=(gx, gy, gz),
                    device_id_type=MESH,
                ).wait_recv()

    @pl.when(from_third)
    def _():
        for s in range(ny):

            @pl.when(jnp.logical_not(jnp.logical_and(gy == 1, jnp.logical_and(gz == 0, s == gy)) & (gz == gy - 1)))
            def _(s=s):
                for c in range(CHUNKS):
                    pltpu.make_async_remote_copy(
                        src_ref=main.at[0, part(c)],
                        dst_ref=got_third.at[s, part(c)],
                        send_sem=send_main.at[0, c],
                        recv_sem=recv_third.at[s, c],
                        device_id=(gx, gy, gz),
                        device_id_type=MESH,
                    ).wait_recv()

            got_main[s] = got_main[s] + got_third[s]

    def add_edge(source, sem, s):
        pltpu.make_async_remote_copy(
            src_ref=edge.at[0],
            dst_ref=source.at[s],
            send_sem=send_edge.at[0],
            recv_sem=sem.at[s],
            device_id=(gx, gy, gz),
            device_id_type=MESH,
        ).wait_recv()
        ghost = jnp.zeros((1, lanes), f32)
        for t in range(subs):
            got_main[s, first_rows[t]] = got_main[s, first_rows[t]] + source[s, t : t + 1]
            moved = source[s, subs + t : subs + t + 1]
            ghost = ghost + (pltpu.roll(jnp.broadcast_to(moved, (8, lanes)), t, 1)[:1] if t else moved)
        last = pl.ds(subs * tile, 1)
        got_main[s, last] = got_main[s, last] + ghost

    @pl.when(from_first)
    def _():
        for s in range(ny):
            add_edge(got_first, recv_first, s)

    @pl.when(from_corner)
    def _():
        for s in range(ny):
            add_edge(got_corner, recv_corner, s)

    lane = iota((tile, lanes), 1)
    lane_y = iota((tile, all_y), 1)
    ghosts = [got_main[s, subs * tile : (subs + 1) * tile] for s in range(ny - 1)]
    bound = [troponin[:, k, :] for k in range(per_block)]
    active = [tension[:, k, :] for k in range(per_block)]
    unbind_rate = [unbind[:, k, :] for k in range(per_block)]
    relax_rate = [relax[:, k, :] for k in range(per_block)]
    for t in range(subs):
        pieces = []
        for s in range(ny):
            value = got_main[s, t * tile : (t + 1) * tile]
            if s:
                moved = pltpu.roll(ghosts[s - 1], lanes - t, 1) if t else ghosts[s - 1]
                value = value + jnp.where(lane % nodes_y == 0, moved, 0.0)
            pieces.append(value)

        def drive(f, k):
            at = (f * per_block + k) * nodes_y
            total = None
            for s in range(ny):
                shift = (s * nodes_y - at) % lanes
                moved = pltpu.roll(pieces[s], shift, 1) if shift else pieces[s]
                total = moved if total is None else jnp.where(lane_y // nodes_y == s, moved, total)
            return total

        for k in range(per_block):
            squared = drive(0, k)
            squared = squared * squared
            binding = squared / (squared + half_square)
            bound[k] = bound[k] + step_size * (
                bind_rate * binding * (1.0 - bound[k]) - unbind_rate[k] * bound[k]
            )
            active[k] = active[k] + step_size * relax_rate[k] * (
                peak_tension * drive(1, k) * bound[k] - active[k]
            )
    for k in range(per_block):
        out_bound[:, k, :] = bound[k]
        out_active[:, k, :] = active[k]

    for c in range(CHUNKS):
        each_main(c, lambda copy: copy.wait_send())
    each_edge(lambda copy: copy.wait_send())


def per_device(calcium, activation, e1, o1, e2, o2, e3, o3, troponin, tension, unbind, relax, *, sizes):
    nx, ny, nz = sizes
    subs, rows, depth, cols = calcium.shape
    nodes_x, per_block, all_y = troponin.shape
    lanes = 2 * per_block * (all_y // ny)
    blocks = nz
    long = (subs + 1) * nodes_x
    vmem = pl.BlockSpec(memory_space=pltpu.VMEM)
    hbm = pl.BlockSpec(memory_space=pltpu.MemorySpace.HBM)
    dma = pltpu.SemaphoreType.DMA
    flat = [x.reshape(1, -1) for x in (e1, o1, e2, o2, e3, o3)]
    shape = jax.ShapeDtypeStruct(troponin.shape, f32)
    return pl.pallas_call(
        functools.partial(kernel, sizes=sizes),
        out_shape=(shape, shape),
        in_specs=[hbm] * 2 + [vmem] * 10,
        out_specs=(vmem, vmem),
        scratch_shapes=[
            pltpu.VMEM(calcium.shape, f32),
            pltpu.VMEM(calcium.shape, f32),
            pltpu.VMEM((blocks + 1, long, lanes), f32),
            pltpu.VMEM((blocks + 1, 2 * subs, lanes), f32),
            pltpu.VMEM((ny, long, lanes), f32),
            pltpu.VMEM((ny, long, lanes), f32),
            pltpu.VMEM((ny, 2 * subs, lanes), f32),
            pltpu.VMEM((ny, 2 * subs, lanes), f32),
            dma((2, subs)),
            dma((blocks + 1, CHUNKS)),
            dma((blocks + 1,)),
            dma((ny, CHUNKS)),
            dma((ny, CHUNKS)),
            dma((ny,)),
            dma((ny,)),
        ],
        compiler_params=pltpu.CompilerParams(
            collective_id=0, has_side_effects=True, vmem_limit_bytes=48 * 1024 * 1024
        ),
        name="restrict_steps",
    )(calcium, activation, *flat, troponin, tension, unbind, relax)


def solution(mesh):
    sizes = tuple(mesh.shape[name] for name in ("gx", "gy", "gz"))
    field = P(None, "gx", "gz", "gy")
    nodes = P("gx", ("gy", "gz"), None)
    return jax.shard_map(
        functools.partial(per_device, sizes=sizes),
        mesh=mesh,
        in_specs=(field, field, P(), P(), P(), P(), P(), P(), nodes, nodes, nodes, nodes),
        out_specs=(nodes, nodes),
        check_vma=False,
    )
```

time: 76.1 us -> 27.5 us (0.36)
  the two profiles are of different devices: /device:TPU:0 before, /device:TPU:7 now
where the time goes in v1:
time: 27.5 us; the launch traced here: 27 us
  Pallas kernels  16.2 us (59%)
  local copies, waits for them, and re-layouts  10.1 us (37%)
  between operations  0.66 us (2%)
    pallas_call x1, Pallas kernels, per_device(): pl.pallas_call(functools.partial(kernel, sizes=sizes), out_shape=(shape,...  16.2 us
    unnamed x24, local copies, waits for them, and re-layouts  10.1 us

profile of v1, /device:TPU:7, one launch (start us, length us, event | category | flops | bytes accessed | tf_op | source)
XLA Modules:
  0.0 27.0 jit_solution(12222891163422414779)
XLA Ops:
  0.6 0.0 copy-start
  0.6 2.2 %copy-done = f32[8,32,32,128]{3,2,1,0:T(8,128)S(1)} copy-done((f32[8,32,32,128]{3,2,1,0:T(8,128)S(1)}, f32[8,32,32,128]{3,2,1,0:T(8,128)}, u32[]{:S(2)}) %copy-start) | copy-done | bytes 4194328
  2.8 0.0 copy-start.1
  2.8 0.7 %copy-done.1 = f32[8,2,128]{2,1,0:T(2,128)S(1)} copy-done((f32[8,2,128]{2,1,0:T(2,128)S(1)}, f32[8,2,128]{2,1,0:T(2,128)}, u32[]{:S(2)}) %copy-start.1) | copy-done | bytes 8216
  3.5 0.0 copy-start.2
  3.5 0.7 %copy-done.2 = f32[8,2,128]{2,1,0:T(2,128)S(1)} copy-done((f32[8,2,128]{2,1,0:T(2,128)S(1)}, f32[8,2,128]{2,1,0:T(2,128)}, u32[]{:S(2)}) %copy-start.2) | copy-done | bytes 8216
  4.2 0.0 copy-start.3
  4.2 0.7 %copy-done.3 = f32[8,2,128]{2,1,0:T(2,128)S(1)} copy-done((f32[8,2,128]{2,1,0:T(2,128)S(1)}, f32[8,2,128]{2,1,0:T(2,128)}, u32[]{:S(2)}) %copy-start.3) | copy-done | bytes 8216
  4.9 0.0 copy-start.4
  4.9 0.7 %copy-done.4 = f32[8,2,128]{2,1,0:T(2,128)S(1)} copy-done((f32[8,2,128]{2,1,0:T(2,128)S(1)}, f32[8,2,128]{2,1,0:T(2,128)}, u32[]{:S(2)}) %copy-start.4) | copy-done | bytes 8216
  5.6 0.0 copy-start.5
  5.6 0.7 %copy-done.5 = s32[512]{0:T(512)S(1)} copy-done((s32[512]{0:T(512)S(1)}, s32[512]{0:T(512)}, u32[]{:S(2)}) %copy-start.5) | copy-done | bytes 2072
  6.3 0.0 copy-start.6
  6.3 0.7 %copy-done.6 = f32[512]{0:T(512)S(1)} copy-done((f32[512]{0:T(512)S(1)}, f32[512]{0:T(512)}, u32[]{:S(2)}) %copy-start.6) | copy-done | bytes 2072
  7.0 0.0 copy-start.7
  7.0 0.7 %copy-done.7 = s32[64]{0:T(128)S(1)} copy-done((s32[64]{0:T(128)S(1)}, s32[64]{0:T(128)}, u32[]{:S(2)}) %copy-start.7) | copy-done | bytes 280
  7.6 0.0 copy-start.8
  7.6 0.7 %copy-done.8 = f32[64]{0:T(128)S(1)} copy-done((f32[64]{0:T(128)S(1)}, f32[64]{0:T(128)}, u32[]{:S(2)}) %copy-start.8) | copy-done | bytes 280
  8.3 0.0 copy-start.9
  8.3 0.7 %copy-done.9 = s32[128]{0:T(128)S(1)} copy-done((s32[128]{0:T(128)S(1)}, s32[128]{0:T(128)}, u32[]{:S(2)}) %copy-start.9) | copy-done | bytes 536
  8.9 0.0 copy-start.10
  8.9 0.7 %copy-done.10 = f32[128]{0:T(128)S(1)} copy-done((f32[128]{0:T(128)S(1)}, f32[128]{0:T(128)}, u32[]{:S(2)}) %copy-start.10) | copy-done | bytes 536
  9.6 16.2 %restrict_steps.1 = (f32[8,2,128]{2,1,0:T(2,128)S(1)}, f32[8,2,128]{2,1,0:T(2,128)S(1)}) custom-call(f32[8,32,32,128]{3,2,1,0:T(8,128)S(1)} %copy-done, f32[8,32,32,128]{3,2,1,0:T(8,128)} %activation.1, s32[1,64]{1,0:T(1,128)S(1)} %bitcast.8, f32[1,64]{1,0:T(1,128)S(1)} %bitcast.9, s32[1,512]{1,0:T(1,128)S(1)} %bitcast.6, f32[1,512]{1,0:T(1,128)S(1)} %bitcast.7, ...), custom_call_target="tpu_custom_call" | custom-call | tf_op jit(solution)/shard_map/restrict_steps/pallas_call | solution.py:421
  25.8 0.6 %copy.16 = f32[8,2,128]{2,1,0:T(2,128)} copy(f32[8,2,128]{2,1,0:T(2,128)S(1)} %get-tuple-element.4) | data formatting | bytes 16384
  26.4 0.6 %copy.17 = f32[8,2,128]{2,1,0:T(2,128)} copy(f32[8,2,128]{2,1,0:T(2,128)S(1)} %get-tuple-element.5) | data formatting | bytes 16384
Async XLA Ops:
  0.6 2.2 %copy-start = (f32[8,32,32,128]{3,2,1,0:T(8,128)S(1)}, f32[8,32,32,128]{3,2,1,0:T(8,128)}, u32[]{:S(2)}) copy-start(f32[8,32,32,128]{3,2,1,0:T(8,128)} %calcium.1) | copy-start | bytes 12582916
  2.8 0.7 %copy-start.1 = (f32[8,2,128]{2,1,0:T(2,128)S(1)}, f32[8,2,128]{2,1,0:T(2,128)}, u32[]{:S(2)}) copy-start(f32[8,2,128]{2,1,0:T(2,128)} %troponin.1) | copy-start | bytes 24580
  3.5 0.7 %copy-start.2 = (f32[8,2,128]{2,1,0:T(2,128)S(1)}, f32[8,2,128]{2,1,0:T(2,128)}, u32[]{:S(2)}) copy-start(f32[8,2,128]{2,1,0:T(2,128)} %tension.1) | copy-start | bytes 24580
  4.2 0.7 %copy-start.3 = (f32[8,2,128]{2,1,0:T(2,128)S(1)}, f32[8,2,128]{2,1,0:T(2,128)}, u32[]{:S(2)}) copy-start(f32[8,2,128]{2,1,0:T(2,128)} %unbind.1) | copy-start | bytes 24580
  4.9 0.7 %copy-start.4 = (f32[8,2,128]{2,1,0:T(2,128)S(1)}, f32[8,2,128]{2,1,0:T(2,128)}, u32[]{:S(2)}) copy-start(f32[8,2,128]{2,1,0:T(2,128)} %relax.1) | copy-start | bytes 24580
  5.6 0.7 %copy-start.5 = (s32[512]{0:T(512)S(1)}, s32[512]{0:T(512)}, u32[]{:S(2)}) copy-start(s32[512]{0:T(512)} %param.16) | copy-start | bytes 6148
  6.3 0.7 %copy-start.6 = (f32[512]{0:T(512)S(1)}, f32[512]{0:T(512)}, u32[]{:S(2)}) copy-start(f32[512]{0:T(512)} %param.17) | copy-start | bytes 6148
  7.0 0.7 %copy-start.7 = (s32[64]{0:T(128)S(1)}, s32[64]{0:T(128)}, u32[]{:S(2)}) copy-start(s32[64]{0:T(128)} %param.14) | copy-start | bytes 772
  7.6 0.7 %copy-start.8 = (f32[64]{0:T(128)S(1)}, f32[64]{0:T(128)}, u32[]{:S(2)}) copy-start(f32[64]{0:T(128)} %param.15) | copy-start | bytes 772
  8.3 0.7 %copy-start.9 = (s32[128]{0:T(128)S(1)}, s32[128]{0:T(128)}, u32[]{:S(2)}) copy-start(s32[128]{0:T(128)} %param.18) | copy-start | bytes 1540
  8.9 0.7 %copy-start.10 = (f32[128]{0:T(128)S(1)}, f32[128]{0:T(128)}, u32[]{:S(2)}) copy-start(f32[128]{0:T(128)} %param.19) | copy-start | bytes 1540

commit v2 on v1

--- a/solution.py
+++ b/solution.py
@@ -30,6 +30,13 @@
     return raw, jnp.where(total > 0.0, total, 1.0)
 
 
+def expand(weight, pick):
+    high, low = split(weight)
+    return jnp.dot(high, pick, preferred_element_type=f32) + jnp.dot(
+        low, pick, preferred_element_type=f32
+    )
+
+
 def iota(shape, dim):
     return lax.broadcasted_iota(jnp.int32, shape, dim)
 
@@ -37,36 +44,30 @@
 def kernel(
     calcium,
     activation,
-    e1,
-    o1,
-    e2,
-    o2,
-    e3,
-    o3,
-    troponin,
-    tension,
-    unbind,
-    relax,
-    out_bound,
-    out_active,
-    xc,
-    xa,
-    main,
-    edge,
-    got_main,
-    got_third,
-    got_first,
-    got_corner,
-    load_sem,
-    send_main,
-    send_edge,
-    recv_main,
-    recv_third,
-    recv_first,
-    recv_corner,
-    *,
+    *refs,
     sizes,
 ):
+    small = refs[:10]
+    out_bound, out_active, xc, xa = refs[10:14]
+    local = refs[14:24]
+    (
+        main,
+        third,
+        edge,
+        got_main,
+        got_third,
+        got_first,
+        got_corner,
+        load_sem,
+        small_sem,
+        send_main,
+        send_edge,
+        recv_main,
+        recv_third,
+        recv_first,
+        recv_corner,
+    ) = refs[24:]
+    e1, o1, e2, o2, e3, o3, troponin, tension, unbind, relax = local
     nx, ny, nz = sizes
     subs, rows, depth, cols = xc.shape
     nodes_x, per_block, all_y = troponin.shape
@@ -82,6 +83,12 @@
             pltpu.make_async_copy(activation.at[t], xa.at[t], load_sem.at[1, t]),
         )
 
+    fetches = [
+        pltpu.make_async_copy(source, target, small_sem.at[i])
+        for i, (source, target) in enumerate(zip(small, local))
+    ]
+    for copy in fetches:
+        copy.start()
     for t in range(subs):
         for copy in load(t):
             copy.start()
@@ -116,6 +123,8 @@
         def _():
             greet(1, 1)
 
+    for copy in fetches[:6]:
+        copy.wait()
     row_count = (slab + 1) * nodes_x + 16
     r = iota((row_count, 1), 0)
     inner = r < (slab + 1) * nodes_x
@@ -126,17 +135,13 @@
     wide = rows * depth
     pick = (
         iota((raw.shape[1], wide), 0) == gx * rows + iota((raw.shape[1], wide), 1) // depth
-    ).astype(f32)
-    weight_x = jnp.dot(
-        raw / total, pick, precision=lax.Precision.HIGHEST, preferred_element_type=f32
-    )
+    ).astype(bf16)
+    weight_x = expand(raw / total, pick)
     raw, total = node_weights(e3[...], o3[...], node_b + gz * slab)
     pick = (
         iota((raw.shape[1], wide), 0) == gz * depth + iota((raw.shape[1], wide), 1) % depth
-    ).astype(f32)
-    weight_z = jnp.dot(
-        raw / total, pick, precision=lax.Precision.HIGHEST, preferred_element_type=f32
-    )
+    ).astype(bf16)
+    weight_z = expand(raw / total, pick)
     k_high, k_low = split(weight_x * weight_z)
     k_both = jnp.concatenate([k_high, k_low], axis=0)
 
@@ -186,10 +191,14 @@
             device_id_type=MESH,
         )
 
+    def third_part(c):
+        step = chunk // per_block * nodes_x
+        return pl.ds(c * step, step + (nodes_x if c == CHUNKS - 1 else 0))
+
     def third_copy(c):
         return pltpu.make_async_remote_copy(
-            src_ref=main.at[blocks, part(c)],
-            dst_ref=got_third.at[gy, part(c)],
+            src_ref=third.at[third_part(c)],
+            dst_ref=got_third.at[gy, third_part(c)],
             send_sem=send_main.at[blocks, c],
             recv_sem=recv_third.at[gy, c],
             device_id=(gx, gz + 1, 0),
@@ -240,7 +249,7 @@
         def _():
             do(corner_copy())
 
-    packed = None
+    packed = pair = None
     tile = nodes_x
     for c in range(CHUNKS):
         gathered = []
@@ -274,18 +283,29 @@
         per = (blocks + 1) * tile + 8
         for k, t in enumerate(range(c * chunk, (c + 1) * chunk)):
             values = result[k * per : (k + 1) * per]
+            for q in range(blocks):
+                main[q, t * tile : (t + 1) * tile] = values[q * tile : (q + 1) * tile, :lanes]
             for q in range(blocks + 1):
-                main[q, t * tile : (t + 1) * tile] = values[q * tile : (q + 1) * tile, :lanes]
                 row = (blocks + 1) * tile + q
                 edge[q, t : t + 1] = values[row : row + 1, :lanes]
-                edge[q, subs + t : subs + t + 1] = values[row : row + 1, lanes:]
-            ghost = values[: (blocks + 1) * tile, lanes:]
+            above = values[blocks * tile : (blocks + 1) * tile, :lanes]
+            place = t % per_block
+            pair = pltpu.roll(above, place * nodes_y, 1) + pair if place else above
+            if place == per_block - 1:
+                at = t // per_block * tile
+                third[at : at + tile] = pair
+            ghost = values[:, lanes:]
             if t:
                 ghost = pltpu.roll(ghost, t, 1)
             packed = ghost if packed is None else packed + ghost
         if c == CHUNKS - 1:
+            for q in range(blocks):
+                main[q, subs * tile : (subs + 1) * tile] = packed[q * tile : (q + 1) * tile]
+            at = subs // per_block * tile
+            third[at : at + tile] = packed[blocks * tile : (blocks + 1) * tile]
             for q in range(blocks + 1):
-                main[q, subs * tile : (subs + 1) * tile] = packed[q * tile : (q + 1) * tile]
+                row = (blocks + 1) * tile + q
+                edge[q, subs : subs + 1] = packed[row : row + 1]
         if c == 0:
             count = blocks + has_next_z.astype(jnp.int32)
             count = count * jnp.where(has_next_x, 2, 1)
@@ -300,9 +320,8 @@
 
     @pl.when(third_here)
     def _():
-        got_third[gy] = main[blocks]
-
-    first_rows = [pl.ds(t * tile, 1) for t in range(subs)]
+        got_third[gy] = third[...]
+
     for s in range(ny):
 
         @pl.when(jnp.logical_not(jnp.logical_and(own, gy == s)))
@@ -325,15 +344,26 @@
             def _(s=s):
                 for c in range(CHUNKS):
                     pltpu.make_async_remote_copy(
-                        src_ref=main.at[0, part(c)],
-                        dst_ref=got_third.at[s, part(c)],
+                        src_ref=third.at[third_part(c)],
+                        dst_ref=got_third.at[s, third_part(c)],
                         send_sem=send_main.at[0, c],
                         recv_sem=recv_third.at[s, c],
                         device_id=(gx, gy, gz),
                         device_id_type=MESH,
                     ).wait_recv()
 
-            got_main[s] = got_main[s] + got_third[s]
+            first_block = iota((tile, lanes), 1) // nodes_y % per_block == 0
+            for t in range(subs):
+                at = t // per_block * tile
+                moved = got_third[s, at : at + tile]
+                place = t % per_block
+                if place:
+                    moved = pltpu.roll(moved, lanes - place * nodes_y, 1)
+                rows_t = pl.ds(t * tile, tile)
+                got_main[s, rows_t] = got_main[s, rows_t] + jnp.where(first_block, moved, 0.0)
+            at = subs // per_block * tile
+            rows_t = pl.ds(subs * tile, tile)
+            got_main[s, rows_t] = got_main[s, rows_t] + got_third[s, at : at + tile]
 
     def add_edge(source, sem, s):
         pltpu.make_async_remote_copy(
@@ -344,13 +374,9 @@
             device_id=(gx, gy, gz),
             device_id_type=MESH,
         ).wait_recv()
-        ghost = jnp.zeros((1, lanes), f32)
-        for t in range(subs):
-            got_main[s, first_rows[t]] = got_main[s, first_rows[t]] + source[s, t : t + 1]
-            moved = source[s, subs + t : subs + t + 1]
-            ghost = ghost + (pltpu.roll(jnp.broadcast_to(moved, (8, lanes)), t, 1)[:1] if t else moved)
-        last = pl.ds(subs * tile, 1)
-        got_main[s, last] = got_main[s, last] + ghost
+        for t in range(subs + 1):
+            at = pl.ds(t * tile, 1)
+            got_main[s, at] = got_main[s, at] + source[s, t : t + 1]
 
     @pl.when(from_first)
     def _():
@@ -362,6 +388,8 @@
         for s in range(ny):
             add_edge(got_corner, recv_corner, s)
 
+    for copy in fetches[6:]:
+        copy.wait()
     lane = iota((tile, lanes), 1)
     lane_y = iota((tile, all_y), 1)
     ghosts = [got_main[s, subs * tile : (subs + 1) * tile] for s in range(ny - 1)]
@@ -406,6 +434,17 @@
     each_edge(lambda copy: copy.wait_send())
 
 
+def store_results(bound, active, out_bound, out_active, sem):
+    copies = (
+        pltpu.make_async_copy(bound, out_bound, sem.at[0]),
+        pltpu.make_async_copy(active, out_active, sem.at[1]),
+    )
+    for copy in copies:
+        copy.start()
+    for copy in copies:
+        copy.wait()
+
+
 def per_device(calcium, activation, e1, o1, e2, o2, e3, o3, troponin, tension, unbind, relax, *, sizes):
     nx, ny, nz = sizes
     subs, rows, depth, cols = calcium.shape
@@ -413,26 +452,34 @@
     lanes = 2 * per_block * (all_y // ny)
     blocks = nz
     long = (subs + 1) * nodes_x
+    short = (subs // per_block + 1) * nodes_x
     vmem = pl.BlockSpec(memory_space=pltpu.VMEM)
     hbm = pl.BlockSpec(memory_space=pltpu.MemorySpace.HBM)
     dma = pltpu.SemaphoreType.DMA
     flat = [x.reshape(1, -1) for x in (e1, o1, e2, o2, e3, o3)]
     shape = jax.ShapeDtypeStruct(troponin.shape, f32)
-    return pl.pallas_call(
+    operands = [
+        pltpu.with_memory_space_constraint(x, pltpu.MemorySpace.HBM)
+        for x in (calcium, activation, *flat, troponin, tension, unbind, relax)
+    ]
+    results = pl.pallas_call(
         functools.partial(kernel, sizes=sizes),
         out_shape=(shape, shape),
-        in_specs=[hbm] * 2 + [vmem] * 10,
+        in_specs=[hbm] * 12,
         out_specs=(vmem, vmem),
         scratch_shapes=[
             pltpu.VMEM(calcium.shape, f32),
             pltpu.VMEM(calcium.shape, f32),
-            pltpu.VMEM((blocks + 1, long, lanes), f32),
-            pltpu.VMEM((blocks + 1, 2 * subs, lanes), f32),
+            *[pltpu.VMEM(x.shape, x.dtype) for x in (*flat, troponin, tension, unbind, relax)],
+            pltpu.VMEM((blocks, long, lanes), f32),
+            pltpu.VMEM((short, lanes), f32),
+            pltpu.VMEM((blocks + 1, subs + 1, lanes), f32),
             pltpu.VMEM((ny, long, lanes), f32),
-            pltpu.VMEM((ny, long, lanes), f32),
-            pltpu.VMEM((ny, 2 * subs, lanes), f32),
-            pltpu.VMEM((ny, 2 * subs, lanes), f32),
+            pltpu.VMEM((ny, short, lanes), f32),
+            pltpu.VMEM((ny, subs + 1, lanes), f32),
+            pltpu.VMEM((ny, subs + 1, lanes), f32),
             dma((2, subs)),
+            dma((10,)),
             dma((blocks + 1, CHUNKS)),
             dma((blocks + 1,)),
             dma((ny, CHUNKS)),
@@ -441,10 +488,19 @@
             dma((ny,)),
         ],
         compiler_params=pltpu.CompilerParams(
-            collective_id=0, has_side_effects=True, vmem_limit_bytes=48 * 1024 * 1024
+            collective_id=0, has_side_effects=True, vmem_limit_bytes=32 * 1024 * 1024
         ),
         name="restrict_steps",
-    )(calcium, activation, *flat, troponin, tension, unbind, relax)
+    )(*operands)
+    results = [pltpu.with_memory_space_constraint(x, pltpu.MemorySpace.VMEM) for x in results]
+    return pl.pallas_call(
+        store_results,
+        out_shape=(shape, shape),
+        in_specs=[vmem] * 2,
+        out_specs=(hbm, hbm),
+        scratch_shapes=[dma((2,))],
+        name="store_results",
+    )(*results)
 
 
 def solution(mesh):

time: 27.5 us -> 18.2 us (0.66); the launches traced: 27 us -> 18 us
  local copies, waits for them, and re-layouts: 10.1 us -> 0 us
  Pallas kernels: 16.2 us -> 17.4 us
    unnamed x24 -> x0, local copies, waits for them, and re-layouts: 10.1 us -> none
    pallas_call x0 -> x1, Pallas kernels: none -> 0.62 us  [per_device(): pl.pallas_call(store_results, out_shape=(shape, shape), in_specs=[vmem] *...]
    pallas_call x1, Pallas kernels: 16.2 us -> 16.8 us  [per_device(): pl.pallas_call(functools.partial(kernel, sizes=sizes), out_shape=(shape,...]
where the time goes in v2:
time: 18.2 us; the launch traced here: 18 us
  Pallas kernels  17.4 us (96%)
  between operations  0.64 us (4%)
    pallas_call x1, Pallas kernels, per_device(): pl.pallas_call(functools.partial(kernel, sizes=sizes), out_shape=(shape,...  16.8 us
    pallas_call x1, Pallas kernels, per_device(): pl.pallas_call(store_results, out_shape=(shape, shape), in_specs=[vmem] *...  0.62 us

profile of v2, /device:TPU:7, one launch (start us, length us, event | category | flops | bytes accessed | tf_op | source)
XLA Modules:
  0.0 18.0 jit_solution(6821359434113020723)
XLA Ops:
  0.6 16.8 %restrict_steps.1 = (f32[8,2,128]{2,1,0:T(2,128)S(1)}, f32[8,2,128]{2,1,0:T(2,128)S(1)}) custom-call(f32[8,32,32,128]{3,2,1,0:T(8,128)} %calcium.1, f32[8,32,32,128]{3,2,1,0:T(8,128)} %activation.1, s32[1,64]{1,0:T(1,128)} %bitcast.8, f32[1,64]{1,0:T(1,128)} %bitcast.9, s32[1,512]{1,0:T(1,128)} %bitcast.6, f32[1,512]{1,0:T(1,128)} %bitcast.7, ...), custom_call_target="tpu_custom_call" | custom-call | tf_op jit(solution)/shard_map/restrict_steps/pallas_call | solution.py:465
  17.4 0.6 %store_results.1 = (f32[8,2,128]{2,1,0:T(2,128)}, f32[8,2,128]{2,1,0:T(2,128)}) custom-call(f32[8,2,128]{2,1,0:T(2,128)S(1)} %get-tuple-element.4.bound, f32[8,2,128]{2,1,0:T(2,128)S(1)} %get-tuple-element.5.active), custom_call_target="tpu_custom_call" | custom-call | tf_op jit(solution)/shard_map/store_results/pallas_call | solution.py:496
